TPU v7x, 256 devices: a whole 4x4x8 slice. The times are simulated.
256 devices in a mesh: seq: 8 (over z), tensor: 8 (over x, y_hi), dp: 4 (over y_lo, core).
Axes of the slice: x: 4, y: 4 (y_hi: 2, y_lo: 2; y = y_hi * 2 + y_lo), z: 8, core: 2. Of those that a mesh axis runs over, the one named last changes fastest.
Arguments:
- tokens: bfloat16 [4, 2048, 3072], P('dp', 'seq'), may hold values from -6 to 6
- cotangent: bfloat16 [4, 2048, 3072], P('dp', 'seq'), may hold values from -6 to 6
- qkv_weight: bfloat16 [3072, 3, 3072], P(('seq', 'dp'), None, 'tensor'), may hold values from -0.109375 to 0.109375
- out_weight: bfloat16 [3072, 3072], P(('seq', 'dp'), 'tensor'), may hold values from -0.109375 to 0.109375
Outputs:
- qkv_grad: float32 [3072, 3, 3072], P(('seq', 'dp'), None, 'tensor')
- out_grad: float32 [3072, 3072], P(('seq', 'dp'), 'tensor')
- branch_grad: bfloat16 [4, 2048, 3072], P('dp', 'seq', 'tensor')
All inputs are finite; a program needn't handle non-finite values.
Results may differ from a plain program's by a relative error of at most 0.025.
Values may be sent and summed in bfloat16 or wider, within the bound.
No kernel may reach another device: no remote copies, remote signals or barrier semaphores. Data moves between devices by JAX's collectives and lax.ppermute only.
A program may use at most 128 MiB of HBM per device.

v0:
```python
import jax
import jax.numpy as jnp
from jax import lax
from jax.sharding import PartitionSpec as P

HD = 128
epsilon = 1e-06


def sent_together(arrays, axis, dim, along):
    both = jnp.concatenate(arrays, axis=along)
    result, at, done = (lax.all_gather(both, axis, axis=dim, tiled=True), 0, [])
    for a in arrays:
        done.append(lax.slice_in_dim(result, at, at + a.shape[along], axis=along))
        at += a.shape[along]
    return tuple(done)


def split_up(shard, dim, size):
    before, after = (shard.shape[:dim], shard.shape[dim + 1 :])
    return jnp.moveaxis(shard.reshape(*before, size, -1, *after), dim, 0)


def summed_on_arrival(shard, axis, dim):
    size = lax.axis_size(axis)
    pieces = lax.all_to_all(split_up(shard, dim, size), axis, 0, 0, tiled=True)
    return jnp.sum(pieces.astype(jnp.float32), axis=0)


def copy_for_each(shard, axis):
    copies = jnp.broadcast_to(shard, (lax.axis_size(axis), *shard.shape))
    return lax.all_to_all(copies, axis, split_axis=0, concat_axis=0, tiled=True)


def taken_together(shard, axis):
    everything = copy_for_each(shard, axis)
    return jnp.sum(everything, axis=0)


def in_one(arrays, axis):
    ends = [0]
    for a in arrays:
        ends.append(ends[-1] + a.size)
    subtotal = taken_together(jnp.concatenate([a.ravel() for a in arrays]), axis)
    return tuple((subtotal[b:e].reshape(a.shape) for a, b, e in zip(arrays, ends, ends[1:])))


def normalize(values):
    average = jnp.mean(values, axis=-1, keepdims=True)
    centered = values - average
    inverse = lax.rsqrt(jnp.mean(centered * centered, axis=-1, keepdims=True) + epsilon)
    return (centered * inverse, inverse)


def normalize_back(gradient, normed, inverse):
    mean_grad = jnp.mean(gradient, axis=-1, keepdims=True)
    mean_both = jnp.mean(gradient * normed, axis=-1, keepdims=True)
    return (gradient - mean_grad - normed * mean_both) * inverse


def local(tokens, cotangent, qkv_weight, out_weight):
    row_count = tokens.shape[1]
    feature_count = tokens.shape[2]
    column_count = out_weight.shape[1]
    head_count = column_count // HD
    score_scale = HD ** (-0.5)
    own_rows = qkv_weight.shape[0]
    grad_rows = cotangent[0]
    normed, inverse = normalize(tokens[0].astype(jnp.float32))
    unit_low = normed.astype(jnp.bfloat16)
    flat_weight = qkv_weight.reshape(own_rows, 3 * column_count)
    piece_qkv, piece_out = sent_together((flat_weight, out_weight), ("seq", "dp"), 0, 1)
    piece_rows = piece_qkv.shape[0]
    left_rows = unit_low
    right_rows = grad_rows
    projected = jnp.dot(left_rows, piece_qkv, preferred_element_type=jnp.float32)
    attended_grad = jnp.dot(right_rows, piece_out, preferred_element_type=jnp.float32)
    full_qkv = piece_qkv
    projected, attended_grad, full_qkv = (projected, attended_grad, full_qkv)
    query_unit, query_inv = normalize(
        projected[:, :column_count].reshape(row_count, head_count, HD)
    )
    key_unit, key_inv = normalize(
        projected[:, column_count : 2 * column_count].reshape(row_count, head_count, HD)
    )
    query_low = query_unit.astype(jnp.bfloat16)
    key_value = jnp.stack(
        [
            key_unit.astype(jnp.bfloat16).reshape(row_count, column_count),
            projected[:, 2 * column_count :].astype(jnp.bfloat16),
        ]
    )
    grad_low = attended_grad.astype(jnp.bfloat16).reshape(row_count, head_count, HD)

    def scores_of(key_rows):
        piece_rows = key_rows.shape[0]
        return (
            jnp.einsum(
                "qhd,khd->hqk",
                query_low,
                key_rows.reshape(piece_rows, head_count, HD),
                preferred_element_type=jnp.float32,
            )
            * score_scale
        )

    every_pair = lax.all_gather(key_value, "seq", axis=1, tiled=True)
    piece_rows = every_pair.shape[1]
    exponent = jnp.exp(scores_of(every_pair[0]))
    add_exp_total = jnp.sum(exponent, axis=-1)
    weighted = jnp.einsum(
        "hqk,khd->qhd",
        exponent.astype(jnp.bfloat16),
        every_pair[1].reshape(piece_rows, head_count, HD),
        preferred_element_type=jnp.float32,
    )
    exp_total, weighted = (add_exp_total, weighted)
    attended_low = (weighted / exp_total.T[:, :, None]).astype(jnp.bfloat16)
    row_delta = jnp.sum(grad_low.astype(jnp.float32) * attended_low.astype(jnp.float32), axis=-1)
    piece_rows = every_pair.shape[1]
    key_rows = every_pair[0].reshape(piece_rows, head_count, HD)
    value_rows = every_pair[1].reshape(piece_rows, head_count, HD)
    probability = jnp.exp(scores_of(every_pair[0])) / exp_total[:, :, None]
    prob_grad = jnp.einsum("qhd,khd->hqk", grad_low, value_rows, preferred_element_type=jnp.float32)
    grad_score = (probability * (prob_grad - row_delta.T[:, :, None]) * score_scale).astype(
        jnp.bfloat16
    )
    query_part = jnp.einsum(
        "hqk,khd->qhd", grad_score, key_rows, preferred_element_type=jnp.float32
    )
    key_part = jnp.einsum("hqk,qhd->khd", grad_score, query_low, preferred_element_type=jnp.float32)
    value_part = jnp.einsum(
        "hqk,qhd->khd",
        probability.astype(jnp.bfloat16),
        grad_low,
        preferred_element_type=jnp.float32,
    )
    every_grad = jnp.stack(
        [key_part.reshape(piece_rows, column_count), value_part.reshape(piece_rows, column_count)]
    )
    pair_grad = lax.psum_scatter(
        every_grad.astype(jnp.bfloat16), "seq", scatter_dimension=1, tiled=True
    ).astype(jnp.float32)
    query_back = normalize_back(query_part, query_unit, query_inv)
    key_back = normalize_back(pair_grad[0].reshape(row_count, head_count, HD), key_unit, key_inv)
    qkv_low = jnp.concatenate(
        [
            query_back.reshape(row_count, column_count),
            key_back.reshape(row_count, column_count),
            pair_grad[1],
        ],
        axis=1,
    ).astype(jnp.bfloat16)
    inner_grad = jnp.einsum("rc,dc->rd", qkv_low, full_qkv, preferred_element_type=jnp.float32)
    attended_flat = attended_low.reshape(row_count, column_count)
    share_width = feature_count // lax.axis_size("tensor")
    own_share = summed_on_arrival(inner_grad.astype(jnp.bfloat16), "tensor", 1)
    offset = lax.axis_index("tensor") * share_width
    unit_own = lax.dynamic_slice_in_dim(normed, offset, share_width, 1)
    row_sums = in_one(
        (
            jnp.sum(own_share, axis=1, keepdims=True),
            jnp.sum(own_share * unit_own, axis=1, keepdims=True),
        ),
        "tensor",
    )
    branch = (
        own_share - row_sums[0] / feature_count - unit_own * (row_sums[1] / feature_count)
    ) * inverse
    left_rows = unit_low
    right_rows = grad_rows
    qkv_term = jnp.einsum(
        "rd,rc->dc", left_rows, qkv_low, preferred_element_type=jnp.float32
    ).reshape(lax.axis_size(("seq", "dp")) * own_rows, 3, column_count)
    out_term = jnp.einsum(
        "rd,rc->dc", right_rows, attended_flat, preferred_element_type=jnp.float32
    )
    summed = lax.psum_scatter(
        jnp.concatenate([qkv_term, out_term[:, None, :]], axis=1).astype(jnp.bfloat16),
        ("seq", "dp"),
        scatter_dimension=0,
        tiled=True,
    ).astype(jnp.float32)
    return (summed[:, :3], summed[:, 3], branch.astype(jnp.bfloat16)[None])


def solution(mesh):
    return jax.shard_map(
        local,
        mesh=mesh,
        in_specs=(
            P("dp", "seq", None),
            P("dp", "seq", None),
            P(("seq", "dp"), None, "tensor"),
            P(("seq", "dp"), "tensor"),
        ),
        out_specs=(
            P(("seq", "dp"), None, "tensor"),
            P(("seq", "dp"), "tensor"),
            P("dp", "seq", "tensor"),
        ),
        check_vma=False,
    )
```

profile of v0, /device:TPU:16, one launch (start us, length us, event | category | flops | bytes accessed | tf_op | source)
XLA Modules:
  0.0 414.2 jit_solution(13253095489150140398)
XLA Ops:
  12.4 73.2 %all-gather.3.cloned.1.call-done = bf16[3072,1536]{1,0:T(8,128)(2,1)} async-done(((bf16[96,1536]{1,0:T(8,128)(2,1)}), bf16[3072,1536]{1,0:T(8,128)(2,1)}) %all-gather.3.cloned.1.call-update) | async-done | bytes 9437200 | tf_op jit(solution)/shard_map/all_gather | solution.py:12
  85.5 5.3 %fusion.2 = f32[256,1152]{1,0:T(8,128)S(1)} fusion(bf16[3072,1536]{1,0:T(8,128)(2,1)} %all-gather.3.cloned.1.call-done, bf16[1,256,3072]{2,1,0:T(8,128)(2,1)S(1)} %copy-done.1, f32[256]{0:T(256)S(1)} %add_rsqrt_fusion.2, f32[256]{0:T(256)S(1)} %broadcast_multiply_fusion.6), kind=kOutput, calls=%fused_computation.5 | convolution fusion | flops 1815085056 | bytes 9832448 | tf_op jit(solution)/shard_map/dot_general | solution.py:76
  104.7 3.2 fusion.38
  107.8 40.1 %all-gather.5.cloned.1.call-done = bf16[2,2048,384]{2,1,0:T(8,128)(2,1)} async-done(((bf16[2,256,384]{2,1,0:T(8,128)(2,1)}), bf16[2,2048,384]{2,1,0:T(8,128)(2,1)}) %all-gather.5.cloned.1.call-update) | async-done | bytes 3145744 | tf_op jit(solution)/shard_map/all_gather | solution.py:107
  147.9 3.9 fusion.64
  151.8 2.6 copy.93
  154.4 2.6 copy.97
  157.0 2.8 fusion.6
  159.8 2.6 fusion.22
  164.3 2.5 multiply_convert_fusion
  170.2 2.6 copy.100
  172.8 2.6 copy.101
  175.4 3.9 pad_maximum_fusion.1
  179.5 3.6 fusion.63
  185.7 3.4 fusion.7
  189.0 36.0 %reduce-scatter.3.cloned.1.call-done = bf16[2,256,384]{2,1,0:T(8,128)(2,1)} async-done(((bf16[2,2048,384]{2,1,0:T(8,128)(2,1)}), bf16[2,256,384]{2,1,0:T(8,128)(2,1)}) %reduce-scatter.3.cloned.1.call-update) | async-done | bytes 393232 | tf_op jit(solution)/shard_map/reduce_scatter | solution.py:141
  240.8 5.7 %convolution_convert_fusion = bf16[3072,3,384]{2,0,1:T(8,128)(2,1)} fusion(bf16[3,384,256]{2,1,0:T(8,128)(2,1)} %bitcast.114, bf16[1,256,3072]{2,1,0:T(8,128)(2,1)S(1)} %copy-done.1, f32[256]{0:T(256)S(1)} %copy-done.14, f32[256]{0:T(256)S(1)} %copy-done.12), kind=kOutput, calls=%fused_computation.7 | convolution fusion | flops 1818624000 | bytes 9242624 | tf_op jit(solution)/shard_map/rd,rc->dc/dot_general | solution.py:172
  246.5 8.4 %pad_maximum_fusion = bf16[3072,4,384]{2,0,1:T(8,128)(2,1)} fusion(bf16[3072,1,384]{2,0,1:T(8,128)(2,1)} %fusion.7, bf16[3072,3,384]{2,0,1:T(8,128)(2,1)} %convolution_convert_fusion), kind=kLoop, calls=%fused_computation | loop fusion | flops 4718592 | bytes 18874368 | tf_op jit(solution)/shard_map/concatenate | solution.py:179
  255.9 5.3 %fusion.8 = bf16[256,3072]{1,0:T(8,128)(2,1)S(1)} fusion(bf16[3072,1536]{1,0:T(8,128)(2,1)} %all-gather.3.cloned.1.call-done, bf16[256,384]{1,0:T(8,128)(2,1)} %get-tuple-element.14, bf16[256,384]{1,0:T(8,128)(2,1)S(1)} %copy-done.8, bf16[256,384]{1,0:T(8,128)(2,1)S(1)} %copy-done.9), kind=kOutput, calls=%fused_computation.18 | convolution fusion | flops 1814495232 | bytes 9240576 | tf_op jit(solution)/shard_map/rc,dc->rd/dot_general | solution.py:154
  262.6 7.3 %all-to-all-start = ((bf16[8,256,384]{2,1,0:T(8,128)(2,1)}), bf16[8,256,384]{2,1,0:T(8,128)(2,1)}, u32[]{:S(2)}, u32[]{:S(2)}) async-start(bf16[8,256,384]{2,1,0:T(8,128)(2,1)} %bitcast.107), calls=%async_computation.2 | async-start | bytes 3145728 | tf_op jit(solution)/shard_map/all_to_all | solution.py:26
  269.9 2.3 fusion.14
  272.2 17.6 %all-to-all-done = bf16[8,256,384]{2,1,0:T(8,128)(2,1)} async-done(((bf16[8,256,384]{2,1,0:T(8,128)(2,1)}), bf16[8,256,384]{2,1,0:T(8,128)(2,1)}, u32[]{:S(2)}, u32[]{:S(2)}) %all-to-all-start) | async-done | bytes 1572896 | tf_op jit(solution)/shard_map/all_to_all | solution.py:26
  292.8 12.0 %all_to_all.11 = f32[8,1,512]{2,1,0:T(1,128)S(1)} all-to-all(f32[8,1,512]{2,1,0:T(1,128)S(1)} %broadcast_in_dim.8), channel_id=1, replica_groups=mesh['seq'=8,'tensor'=8,'dp'=4] {'tensor'}, dimensions={0} | all-to-all | bytes 32768 | tf_op jit(solution)/shard_map/all_to_all | solution.py:32
  306.7 97.6 %reduce-scatter.5.cloned.1.call-done = bf16[96,4,384]{2,0,1:T(8,128)(2,1)} async-done(((bf16[3072,4,384]{2,0,1:T(8,128)(2,1)}), bf16[96,4,384]{2,0,1:T(8,128)(2,1)}) %reduce-scatter.5.cloned.1.call-update) | async-done | bytes 294928 | tf_op jit(solution)/shard_map/reduce_scatter | solution.py:178
  (89 shorter events, 53.2 us)
Async XLA Ops:
  7.2 97.5 %copy-start = (bf16[1,256,3072]{2,1,0:T(8,128)(2,1)S(1)}, bf16[1,256,3072]{2,1,0:T(8,128)(2,1)}, u32[]{:S(2)}) copy-start(bf16[1,256,3072]{2,1,0:T(8,128)(2,1)} %param.5) | copy-start | bytes 4718596
  7.2 4.6 %copy-start.1 = (bf16[1,256,3072]{2,1,0:T(8,128)(2,1)S(1)}, bf16[1,256,3072]{2,1,0:T(8,128)(2,1)}, u32[]{:S(2)}) copy-start(bf16[1,256,3072]{2,1,0:T(8,128)(2,1)} %param.4) | copy-start | bytes 4718596
  7.2 78.3 %all-gather.3.cloned.1.call-start = ((), (), s32[]{:S(2)}) async-start(), calls=%async_computation.4 | async-start | bytes 9732096 | tf_op jit(solution)/shard_map/all_gather | solution.py:12
  10.0 137.9 %all-gather.5.cloned.1.call-start = ((), (), s32[]{:S(2)}) async-start(), calls=%async_computation.5 | async-start | bytes 3538944 | tf_op jit(solution)/shard_map/all_gather | solution.py:107
  11.8 79.0 %copy-start.11 = (f32[256]{0:T(256)}, f32[256]{0:T(256)S(1)}, u32[]{:S(2)}) copy-start(f32[256]{0:T(256)S(1)} %broadcast_multiply_fusion.6) | copy-start | bytes 3076
  12.3 78.4 %copy-start.13 = (f32[256]{0:T(256)}, f32[256]{0:T(256)S(1)}, u32[]{:S(2)}) copy-start(f32[256]{0:T(256)S(1)} %add_rsqrt_fusion.2) | copy-start | bytes 3076
  90.8 1.2 copy-start.6
  93.8 9.5 %copy-start.4 = (f32[256,384]{0,1:T(8,128)}, f32[256,384]{0,1:T(8,128)S(1)}, u32[]{:S(2)}) copy-start(f32[256,384]{0,1:T(8,128)S(1)} %copy.90) | copy-start | bytes 1179652
  103.3 121.7 %reduce-scatter.3.cloned.1.call-start = ((), (), s32[]{:S(2)}) async-start(), calls=%async_computation.6 | async-start | bytes 3538944 | tf_op jit(solution)/shard_map/reduce_scatter | solution.py:141
  157.0 2.8 copy-start.10
  159.8 2.6 copy-start.3
  166.8 1.6 copy-start.2
  179.3 225.0 %reduce-scatter.5.cloned.1.call-start = ((), (), s32[]{:S(2)}) async-start(), calls=%async_computation.7 | async-start | bytes 9732096 | tf_op jit(solution)/shard_map/reduce_scatter | solution.py:178
  183.9 44.9 %copy-start.5 = (f32[256,384]{0,1:T(8,128)S(1)}, f32[256,384]{0,1:T(8,128)}, u32[]{:S(2)}) copy-start(f32[256,384]{0,1:T(8,128)} %copy-done.4) | copy-start | bytes 1179652
  231.9 8.9 %copy-start.12 = (f32[256]{0:T(256)S(1)}, f32[256]{0:T(256)}, u32[]{:S(2)}) copy-start(f32[256]{0:T(256)} %copy-done.11) | copy-start | bytes 3076
  231.9 8.9 %copy-start.14 = (f32[256]{0:T(256)S(1)}, f32[256]{0:T(256)}, u32[]{:S(2)}) copy-start(f32[256]{0:T(256)} %copy-done.13) | copy-start | bytes 3076
  236.1 0.7 copy-start.7
  254.9 0.9 copy-start.8
  254.9 1.0 copy-start.9
  262.6 27.2 %all-to-all-start = ((bf16[8,256,384]{2,1,0:T(8,128)(2,1)}), bf16[8,256,384]{2,1,0:T(8,128)(2,1)}, u32[]{:S(2)}, u32[]{:S(2)}) async-start(bf16[8,256,384]{2,1,0:T(8,128)(2,1)} %bitcast.107), calls=%async_computation.2 | async-start | bytes 3145728 | tf_op jit(solution)/shard_map/all_to_all | solution.py:26
Sparse Core Ops, SparseCore 0:
  10.4 75.0 all-gather.2
  103.4 44.4 all-gather.4
  179.4 45.5 reduce-scatter.2
  255.1 149.1 reduce-scatter.4
where the time goes:
time: 415 us; the launch traced here: 414 us
  waiting for transfers between devices  264 us (64%)
  local copies, waits for them, and re-layouts  42.5 us (10%)
  matrix products  37.9 us (9%)
  other arithmetic  35.6 us (9%)
  between operations  14 us (3%)
  blocking collectives  12 us (3%)
  starting transfers between devices  7.64 us (2%)
    reduce_scatter x1, waiting for transfers between devices, local(): lax.psum_scatter(jnp.concatenate([qkv_term, out_term[:, None, :]], axis=1...  97.6 us
    all_gather x1, waiting for transfers between devices, sent_together(): result, at, done = (lax.all_gather(both, axis, axis=dim, tiled=True), 0, [])  73.2 us
    all_gather x1, waiting for transfers between devices, local(): every_pair = lax.all_gather(key_value, 'seq', axis=1, tiled=True)  40.1 us
    reduce_scatter x1, waiting for transfers between devices, local(): lax.psum_scatter(every_grad.astype(jnp.bfloat16), 'seq', scatter_dimensio...  36 us
    all_to_all x1, waiting for transfers between devices, summed_on_arrival(): pieces = lax.all_to_all(split_up(shard, dim, size), axis, 0, 0, tiled=True)  17.6 us
    all_to_all x1, blocking collectives, copy_for_each(): return lax.all_to_all(copies, axis, split_axis=0, concat_axis=0, tiled=True)  12 us
    concatenate x1, other arithmetic, local(): jnp.concatenate([qkv_term, out_term[:, None, :]], axis=1)  8.45 us
  transfers between devices with their start and end apart: 5, of which 5 were waited for; matrix products, arithmetic and copies ran while one was open for 7% of the time, Pallas kernels for 0%

commit v1 on v0

--- a/solution.py
+++ b/solution.py
@@ -104,7 +104,7 @@
             * score_scale
         )
 
-    every_pair = lax.all_gather(key_value, "seq", axis=1, tiled=True)
+    every_pair = jnp.concatenate(lax.all_gather(key_value, "seq"), axis=1)
     piece_rows = every_pair.shape[1]
     exponent = jnp.exp(scores_of(every_pair[0]))
     add_exp_total = jnp.sum(exponent, axis=-1)

time: 415 us -> 423 us (1.019)
  local copies, waits for them, and re-layouts: 42.5 us -> 49.8 us
    another operation x0 -> x2, local copies, waits for them, and re-layouts: none -> 7.5 us  [the longest x1 3.76 us: local(): value_rows = every_pair[1].reshape(piece_rows, head_count, HD)]
    all_gather x0 -> x1, local copies, waits for them, and re-layouts: none -> 5.13 us  [local(): every_pair = jnp.concatenate(lax.all_gather(key_value, 'seq'), axis=1)]
where the time goes in v1:
time: 423 us; the launch traced here: 421 us
  waiting for transfers between devices  264 us (62%)
  local copies, waits for them, and re-layouts  49.8 us (12%)
  matrix products  37.9 us (9%)
  other arithmetic  35.6 us (8%)
  between operations  14 us (3%)
  blocking collectives  11.8 us (3%)
  starting transfers between devices  7.78 us (2%)
    reduce_scatter x1, waiting for transfers between devices, local(): lax.psum_scatter(jnp.concatenate([qkv_term, out_term[:, None, :]], axis=1...  97 us
    all_gather x1, waiting for transfers between devices, sent_together(): result, at, done = (lax.all_gather(both, axis, axis=dim, tiled=True), 0, [])  73.2 us
    all_gather x1, waiting for transfers between devices, local(): every_pair = jnp.concatenate(lax.all_gather(key_value, 'seq'), axis=1)  39.9 us
    reduce_scatter x1, waiting for transfers between devices, local(): lax.psum_scatter(every_grad.astype(jnp.bfloat16), 'seq', scatter_dimensio...  35.9 us
    all_to_all x1, waiting for transfers between devices, summed_on_arrival(): pieces = lax.all_to_all(split_up(shard, dim, size), axis, 0, 0, tiled=True)  17.9 us
    all_to_all x1, blocking collectives, copy_for_each(): return lax.all_to_all(copies, axis, split_axis=0, concat_axis=0, tiled=True)  11.8 us
  transfers between devices with their start and end apart: 5, of which 5 were waited for; matrix products, arithmetic and copies ran while one was open for 7% of the time, Pallas kernels for 0%

profile of v1, /device:TPU:16, one launch (start us, length us, event | category | flops | bytes accessed | tf_op | source)
XLA Modules:
  0.0 420.9 jit_solution(4001057362221535600)
XLA Ops:
  12.4 73.2 %all-gather.4.cloned.1.call-done = bf16[3072,1536]{1,0:T(8,128)(2,1)} async-done(((bf16[96,1536]{1,0:T(8,128)(2,1)}), bf16[3072,1536]{1,0:T(8,128)(2,1)}) %all-gather.4.cloned.1.call-update) | async-done | bytes 9437200 | tf_op jit(solution)/shard_map/all_gather | solution.py:12
  85.5 5.3 %fusion.2 = f32[256,1152]{1,0:T(8,128)S(1)} fusion(bf16[3072,1536]{1,0:T(8,128)(2,1)} %all-gather.4.cloned.1.call-done, bf16[1,256,3072]{2,1,0:T(8,128)(2,1)S(1)} %copy-done.1, f32[256]{0:T(256)S(1)} %add_rsqrt_fusion.2, f32[256]{0:T(256)S(1)} %broadcast_multiply_fusion.6), kind=kOutput, calls=%fused_computation.5 | convolution fusion | flops 1815085056 | bytes 9832448 | tf_op jit(solution)/shard_map/dot_general | solution.py:76
  104.8 3.2 fusion.38
  108.0 39.9 %all-gather.6.cloned.1.call-done = bf16[16,256,384]{2,1,0:T(8,128)(2,1)} async-done(((bf16[2,256,384]{2,1,0:T(8,128)(2,1)}), bf16[16,256,384]{2,1,0:T(8,128)(2,1)}) %all-gather.6.cloned.1.call-update) | async-done | bytes 3145744 | tf_op jit(solution)/shard_map/all_gather | solution.py:107
  147.9 5.1 %copy.88 = bf16[8,2,256,384]{2,0,3,1:T(8,128)(2,1)} copy(bf16[8,2,256,384]{3,2,1,0:T(8,128)(2,1)} %bitcast.119) | data formatting | bytes 6291456 | tf_op jit(solution)/shard_map/all_gather | solution.py:107
  153.0 3.8 fusion.64
  156.8 3.7 reshape_squeeze.14
  160.5 3.8 reshape_squeeze.15
  164.3 2.8 fusion.6
  167.1 2.6 fusion.22
  171.5 2.5 multiply_convert_fusion
  177.4 2.6 copy.94
  180.1 2.6 copy.95
  182.6 3.9 pad_maximum_fusion.1
  186.8 3.6 fusion.63
  193.0 3.4 fusion.7
  196.4 35.9 %reduce-scatter.3.cloned.1.call-done = bf16[2,256,384]{2,1,0:T(8,128)(2,1)} async-done(((bf16[2,2048,384]{2,1,0:T(8,128)(2,1)}), bf16[2,256,384]{2,1,0:T(8,128)(2,1)}) %reduce-scatter.3.cloned.1.call-update) | async-done | bytes 393232 | tf_op jit(solution)/shard_map/reduce_scatter | solution.py:141
  248.1 5.7 %convolution_convert_fusion = bf16[3072,3,384]{2,0,1:T(8,128)(2,1)} fusion(bf16[3,384,256]{2,1,0:T(8,128)(2,1)} %bitcast.120, bf16[1,256,3072]{2,1,0:T(8,128)(2,1)S(1)} %copy-done.1, f32[256]{0:T(256)S(1)} %copy-done.14, f32[256]{0:T(256)S(1)} %copy-done.12), kind=kOutput, calls=%fused_computation.7 | convolution fusion | flops 1818624000 | bytes 9242624 | tf_op jit(solution)/shard_map/rd,rc->dc/dot_general | solution.py:172
  253.7 8.4 %pad_maximum_fusion = bf16[3072,4,384]{2,0,1:T(8,128)(2,1)} fusion(bf16[3072,1,384]{2,0,1:T(8,128)(2,1)} %fusion.7, bf16[3072,3,384]{2,0,1:T(8,128)(2,1)} %convolution_convert_fusion), kind=kLoop, calls=%fused_computation | loop fusion | flops 4718592 | bytes 18874368 | tf_op jit(solution)/shard_map/concatenate | solution.py:179
  263.2 5.3 %fusion.8 = bf16[256,3072]{1,0:T(8,128)(2,1)S(1)} fusion(bf16[3072,1536]{1,0:T(8,128)(2,1)} %all-gather.4.cloned.1.call-done, bf16[256,384]{1,0:T(8,128)(2,1)} %get-tuple-element.14, bf16[256,384]{1,0:T(8,128)(2,1)S(1)} %copy-done.8, bf16[256,384]{1,0:T(8,128)(2,1)S(1)} %copy-done.9), kind=kOutput, calls=%fused_computation.18 | convolution fusion | flops 1814495232 | bytes 9240576 | tf_op jit(solution)/shard_map/rc,dc->rd/dot_general | solution.py:154
  269.9 7.2 %all-to-all-start = ((bf16[8,256,384]{2,1,0:T(8,128)(2,1)}), bf16[8,256,384]{2,1,0:T(8,128)(2,1)}, u32[]{:S(2)}, u32[]{:S(2)}) async-start(bf16[8,256,384]{2,1,0:T(8,128)(2,1)} %bitcast.114), calls=%async_computation.2 | async-start | bytes 3145728 | tf_op jit(solution)/shard_map/all_to_all | solution.py:26
  279.4 17.9 %all-to-all-done = bf16[8,256,384]{2,1,0:T(8,128)(2,1)} async-done(((bf16[8,256,384]{2,1,0:T(8,128)(2,1)}), bf16[8,256,384]{2,1,0:T(8,128)(2,1)}, u32[]{:S(2)}, u32[]{:S(2)}) %all-to-all-start) | async-done | bytes 1572896 | tf_op jit(solution)/shard_map/all_to_all | solution.py:26
  300.2 11.8 %all_to_all.11 = f32[8,1,512]{2,1,0:T(1,128)S(1)} all-to-all(f32[8,1,512]{2,1,0:T(1,128)S(1)} %broadcast_in_dim.8), channel_id=1, replica_groups=mesh['seq'=8,'tensor'=8,'dp'=4] {'tensor'}, dimensions={0} | all-to-all | bytes 32768 | tf_op jit(solution)/shard_map/all_to_all | solution.py:32
  313.9 97.0 %reduce-scatter.5.cloned.1.call-done = bf16[96,4,384]{2,0,1:T(8,128)(2,1)} async-done(((bf16[3072,4,384]{2,0,1:T(8,128)(2,1)}), bf16[96,4,384]{2,0,1:T(8,128)(2,1)}) %reduce-scatter.5.cloned.1.call-update) | async-done | bytes 294928 | tf_op jit(solution)/shard_map/reduce_scatter | solution.py:178
  (90 shorter events, 55.7 us)
Async XLA Ops:
  7.2 97.6 %copy-start = (bf16[1,256,3072]{2,1,0:T(8,128)(2,1)S(1)}, bf16[1,256,3072]{2,1,0:T(8,128)(2,1)}, u32[]{:S(2)}) copy-start(bf16[1,256,3072]{2,1,0:T(8,128)(2,1)} %param.5) | copy-start | bytes 4718596
  7.2 4.6 %copy-start.1 = (bf16[1,256,3072]{2,1,0:T(8,128)(2,1)S(1)}, bf16[1,256,3072]{2,1,0:T(8,128)(2,1)}, u32[]{:S(2)}) copy-start(bf16[1,256,3072]{2,1,0:T(8,128)(2,1)} %param.4) | copy-start | bytes 4718596
  7.2 78.3 %all-gather.4.cloned.1.call-start = ((), (), s32[]{:S(2)}) async-start(), calls=%async_computation.4 | async-start | bytes 9732096 | tf_op jit(solution)/shard_map/all_gather | solution.py:12
  10.0 137.9 %all-gather.6.cloned.1.call-start = ((), (), s32[]{:S(2)}) async-start(), calls=%async_computation.7 | async-start | bytes 3538944 | tf_op jit(solution)/shard_map/all_gather | solution.py:107
  11.8 79.0 %copy-start.11 = (f32[256]{0:T(256)}, f32[256]{0:T(256)S(1)}, u32[]{:S(2)}) copy-start(f32[256]{0:T(256)S(1)} %broadcast_multiply_fusion.6) | copy-start | bytes 3076
  12.3 78.4 %copy-start.13 = (f32[256]{0:T(256)}, f32[256]{0:T(256)S(1)}, u32[]{:S(2)}) copy-start(f32[256]{0:T(256)S(1)} %add_rsqrt_fusion.2) | copy-start | bytes 3076
  90.8 1.2 copy-start.6
  93.8 9.4 %copy-start.4 = (f32[256,384]{0,1:T(8,128)}, f32[256,384]{0,1:T(8,128)S(1)}, u32[]{:S(2)}) copy-start(f32[256,384]{0,1:T(8,128)S(1)} %copy.85) | copy-start | bytes 1179652
  103.3 129.0 %reduce-scatter.3.cloned.1.call-start = ((), (), s32[]{:S(2)}) async-start(), calls=%async_computation.5 | async-start | bytes 3538944 | tf_op jit(solution)/shard_map/reduce_scatter | solution.py:141
  164.3 2.8 copy-start.10
  167.1 2.6 copy-start.3
  174.1 1.6 copy-start.2
  186.6 224.4 %reduce-scatter.5.cloned.1.call-start = ((), (), s32[]{:S(2)}) async-start(), calls=%async_computation.6 | async-start | bytes 9732096 | tf_op jit(solution)/shard_map/reduce_scatter | solution.py:178
  191.2 44.9 %copy-start.5 = (f32[256,384]{0,1:T(8,128)S(1)}, f32[256,384]{0,1:T(8,128)}, u32[]{:S(2)}) copy-start(f32[256,384]{0,1:T(8,128)} %copy-done.4) | copy-start | bytes 1179652
  239.1 8.9 %copy-start.12 = (f32[256]{0:T(256)S(1)}, f32[256]{0:T(256)}, u32[]{:S(2)}) copy-start(f32[256]{0:T(256)} %copy-done.11) | copy-start | bytes 3076
  239.1 8.9 %copy-start.14 = (f32[256]{0:T(256)S(1)}, f32[256]{0:T(256)}, u32[]{:S(2)}) copy-start(f32[256]{0:T(256)} %copy-done.13) | copy-start | bytes 3076
  243.4 0.7 copy-start.7
  262.2 0.9 copy-start.8
  262.2 1.0 copy-start.9
  269.9 27.3 %all-to-all-start = ((bf16[8,256,384]{2,1,0:T(8,128)(2,1)}), bf16[8,256,384]{2,1,0:T(8,128)(2,1)}, u32[]{:S(2)}, u32[]{:S(2)}) async-start(bf16[8,256,384]{2,1,0:T(8,128)(2,1)} %bitcast.114), calls=%async_computation.2 | async-start | bytes 3145728 | tf_op jit(solution)/shard_map/all_to_all | solution.py:26
Sparse Core Ops, SparseCore 0:
  10.4 75.0 all-gather.3
  103.4 44.4 all-gather.5
  186.7 45.5 reduce-scatter.2
  262.3 148.5 reduce-scatter.4
